TPU v7x, 256 devices: a whole 4x4x8 slice. The times are simulated.
256 devices in a mesh: tm: 16 (over y, z_hi), lat: 4 (over z_lo, core), lon: 4 (over x).
Axes of the slice: x: 4, y: 4, z: 8 (z_hi: 4, z_lo: 2; z = z_hi * 2 + z_lo), core: 2. Of those that a mesh axis runs over, the one named last changes fastest.
Arguments:
- anomaly: bfloat16 [1024, 294912], P('tm', ('lat', 'lon')), may hold values from -40 to 40, as said below
- start_basis: bfloat16 [64, 294912], P(None, ('lat', 'lon')), may hold values from -0.01171875 to 0.01171875
Outputs:
- eof_basis: bfloat16 [64, 294912], P(None, ('lat', 'lon'))
- factor_diag: float32 [64], replicated
Inputs may be any that keep to these rules, and one draw needn't show every extreme that they name: `anomaly`: Real-valued anomalies whose magnitude varies between hours, latitude rows and longitude columns.
All inputs are finite; a program needn't handle non-finite values.
Results may differ from a plain program's by a relative error of at most 0.035.
Values may be sent and summed in bfloat16 or wider, within the bound.
No kernel may reach another device: no remote copies, remote signals or barrier semaphores. Data moves between devices by JAX's collectives and lax.ppermute only.
A program may use at most 64 MiB of HBM per device.

v0:
```python
import jax
import jax.numpy as jnp
from jax import lax
from jax.sharding import PartitionSpec as P

ITERS = 3
NLAT = 384
NLON = 768


def sent_to_all(shard, axis):
    count = lax.axis_size(axis)
    return lax.all_to_all(
        jnp.broadcast_to(shard[None], (count, *shard.shape)), axis, 0, 0, tiled=True
    )


def over_copies(shard, axis):
    return sent_to_all(shard, axis).sum(axis=0)


def padded_to(lines, count):
    spare = -lines.shape[0] % count
    if not spare:
        return lines
    return jnp.concatenate([lines, jnp.zeros((spare, *lines.shape[1:]), lines.dtype)])


def laid_out(parts, dim):
    lengths = list(parts.shape[1:])
    lengths[dim] *= parts.shape[0]
    return jnp.moveaxis(parts, 0, dim).reshape(lengths)


def collect(shard, axis, dim):
    return laid_out(sent_to_all(shard, axis), dim)


def in_blocks(shard, dim, count):
    before, after = (shard.shape[:dim], shard.shape[dim + 1 :])
    return jnp.moveaxis(shard.reshape(*before, count, -1, *after), dim, 0)


def sum_at_owner(shard, axis, dim):
    parts = in_blocks(shard, dim, lax.axis_size(axis))
    arrived = lax.all_to_all(parts, axis, split_axis=0, concat_axis=0, tiled=True)
    return arrived.astype(jnp.float32).sum(axis=0)


def nested_sum(shard, axes):
    lines = shard.reshape(-1, shard.shape[-1])
    padded = padded_to(lines, lax.axis_size(axes))
    whole = collect(sum_at_owner(padded, axes, 0).astype(jnp.bfloat16), axes, 0)
    return lax.slice_in_dim(whole, 0, len(lines)).reshape(shard.shape).astype(jnp.float32)


def local(anomaly, start_basis):
    hour_rows, points = anomaly.shape
    basis_rank = start_basis.shape[0]
    total_hours = hour_rows * lax.axis_size("tm")
    block_index = lax.axis_index("lat") * lax.axis_size("lon") + lax.axis_index("lon")
    global_point = block_index * points + jnp.arange(points, dtype=jnp.int32)
    lat_index = global_point // NLON
    latitude = (-90.0 + 180.0 * (lat_index.astype(jnp.float32) + 0.5) / NLAT) * (jnp.pi / 180.0)
    weight_row = jnp.sqrt(jnp.cos(latitude))
    current = start_basis
    factor = jnp.zeros((basis_rank, basis_rank), jnp.float32)
    for iteration in range(ITERS):
        scaled = (current.astype(jnp.float32) * weight_row).astype(jnp.bfloat16)
        local_coeffs = lax.dot_general(
            anomaly, scaled, (((1,), (1,)), ((), ())), preferred_element_type=jnp.float32
        )
        coeffs = over_copies(local_coeffs, ("lat", "lon")).astype(jnp.bfloat16)
        partial_value = lax.dot_general(
            coeffs, anomaly, (((0,), (0,)), ((), ())), preferred_element_type=jnp.float32
        )
        summed = nested_sum(partial_value.astype(jnp.bfloat16), "tm")
        image = summed * weight_row / total_hours
        local_gram = jnp.dot(image, image.T, precision=lax.Precision.HIGHEST)
        gram_sum = over_copies(local_gram, ("lat", "lon"))
        factor = jnp.linalg.cholesky(gram_sum)
        solved = lax.linalg.triangular_solve(factor, image, left_side=True, lower=True)
        current = solved.astype(jnp.bfloat16)
    return (current, jnp.diagonal(factor))


def solution(mesh):
    in_specs = (P("tm", ("lat", "lon")), P(None, ("lat", "lon")))
    out_specs = (P(None, ("lat", "lon")), P())
    return jax.shard_map(local, mesh=mesh, in_specs=in_specs, out_specs=out_specs, check_vma=False)
```

profile of v0, /device:TPU:1, one launch (start us, length us, event | category | flops | bytes accessed | tf_op | source)
XLA Modules:
  0.0 608.5 jit_solution(17154272074576143813)
XLA Ops:
  5.2 14.4 %all_to_all.60 = f32[16,1,4096]{2,1,0:T(1,128)S(1)} all-to-all(f32[16,1,4096]{2,1,0:T(1,128)S(1)} %reshape.119), channel_id=1, replica_groups=mesh['tm'=16,'lat'=4,'lon'=4] {'lat','lon'}, dimensions={0} | all-to-all | bytes 524288 | tf_op jit(solution)/shard_map/all_to_all | solution.py:13
  23.9 4.2 reshape.97
  28.1 67.4 %all_to_all.61 = bf16[16,4,18432]{2,1,0:T(4,128)(2,1)} all-to-all(bf16[16,4,18432]{2,1,0:T(4,128)(2,1)} %reshape.97), channel_id=1, replica_groups=mesh['tm'=16,'lat'=4,'lon'=4] {'tm'}, dimensions={0} | all-to-all | bytes 4718592 | tf_op jit(solution)/shard_map/all_to_all | solution.py:46
  99.2 55.9 %all_to_all.62 = bf16[16,4,18432]{2,1,0:T(4,128)(2,1)S(1)} all-to-all(bf16[16,4,18432]{2,1,0:T(4,128)(2,1)S(1)} %broadcast_in_dim.22), channel_id=1, replica_groups=mesh['tm'=16,'lat'=4,'lon'=4] {'tm'}, dimensions={0} | all-to-all | bytes 4718592 | tf_op jit(solution)/shard_map/all_to_all | solution.py:13
  160.0 5.7 div.47
  165.7 7.6 %fusion.49 = f32[64,64]{1,0:T(8,128)S(1)} fusion(f32[64,18432]{1,0:T(8,128)} %div.47), kind=kOutput, calls=%fused_computation.78 | convolution fusion | flops 905969664 | bytes 4734976 | tf_op jit(solution)/shard_map/dot_general | solution.py:79
  174.4 8.0 %all-to-all-start.3 = ((f32[16,1,4096]{2,1,0:T(1,128)}), f32[16,1,4096]{2,1,0:T(1,128)S(1)}, u32[]{:S(2)}, u32[]{:S(2)}) async-start(f32[16,1,4096]{2,1,0:T(1,128)} %reshape.121), calls=%async_computation.3 | async-start | bytes 524288 | tf_op jit(solution)/shard_map/all_to_all | solution.py:13
  182.5 4.3 reshape.104
  191.6 5.8 cholesky.59
  198.7 4.9 custom-call.9
  203.6 6.7 %fusion.5 = bf16[64,18432]{1,0:T(8,128)(2,1)S(1)} fusion(f32[64,18432]{1,0:T(8,128)} %reshape.104, f32[18432]{0:T(1024)S(1)} %fusion.27, f32[1,64,64]{1,2,0:T(8,128)S(1)} %custom-call.9), kind=kOutput, calls=%fused_computation.11 | convolution fusion | flops 913047552 | bytes 7168000 | tf_op jit(solution)/shard_map/triangular_solve/dot.1 | solution.py:82
  211.6 10.7 %all_to_all.63 = f32[16,1,4096]{2,1,0:T(1,128)S(1)} all-to-all(f32[16,1,4096]{2,1,0:T(1,128)S(1)} %reshape.123), channel_id=1, replica_groups=mesh['tm'=16,'lat'=4,'lon'=4] {'lat','lon'}, dimensions={0} | all-to-all | bytes 524288 | tf_op jit(solution)/shard_map/all_to_all | solution.py:13
  226.0 4.2 reshape.98
  230.2 62.3 %all_to_all.64 = bf16[16,4,18432]{2,1,0:T(4,128)(2,1)} all-to-all(bf16[16,4,18432]{2,1,0:T(4,128)(2,1)} %reshape.98), channel_id=1, replica_groups=mesh['tm'=16,'lat'=4,'lon'=4] {'tm'}, dimensions={0} | all-to-all | bytes 4718592 | tf_op jit(solution)/shard_map/all_to_all | solution.py:46
  296.2 59.4 %all_to_all.65 = bf16[16,4,18432]{2,1,0:T(4,128)(2,1)S(1)} all-to-all(bf16[16,4,18432]{2,1,0:T(4,128)(2,1)S(1)} %broadcast_in_dim.25), channel_id=1, replica_groups=mesh['tm'=16,'lat'=4,'lon'=4] {'tm'}, dimensions={0} | all-to-all | bytes 4718592 | tf_op jit(solution)/shard_map/all_to_all | solution.py:13
  360.5 5.7 div.50
  366.2 7.6 %fusion.50 = f32[64,64]{1,0:T(8,128)S(1)} fusion(f32[64,18432]{1,0:T(8,128)} %div.50), kind=kOutput, calls=%fused_computation.79 | convolution fusion | flops 905969664 | bytes 4734976 | tf_op jit(solution)/shard_map/dot_general | solution.py:79
  375.0 5.2 all-to-all-start.7
  380.2 4.3 reshape.105
  389.3 5.8 cholesky.70
  396.5 4.9 custom-call.10
  401.4 6.7 %fusion.2 = bf16[64,18432]{1,0:T(8,128)(2,1)S(1)} fusion(f32[64,18432]{1,0:T(8,128)} %reshape.105, f32[18432]{0:T(1024)S(1)} %fusion.27, f32[1,64,64]{1,2,0:T(8,128)S(1)} %custom-call.10), kind=kOutput, calls=%fused_computation.6 | convolution fusion | flops 913047552 | bytes 7168000 | tf_op jit(solution)/shard_map/triangular_solve/dot.1 | solution.py:82
  409.3 10.7 %all_to_all.66 = f32[16,1,4096]{2,1,0:T(1,128)S(1)} all-to-all(f32[16,1,4096]{2,1,0:T(1,128)S(1)} %reshape.127), channel_id=1, replica_groups=mesh['tm'=16,'lat'=4,'lon'=4] {'lat','lon'}, dimensions={0} | all-to-all | bytes 524288 | tf_op jit(solution)/shard_map/all_to_all | solution.py:13
  428.0 62.1 %all_to_all.67 = bf16[16,4,18432]{2,1,0:T(4,128)(2,1)} all-to-all(bf16[16,4,18432]{2,1,0:T(4,128)(2,1)} %reshape.99), channel_id=1, replica_groups=mesh['tm'=16,'lat'=4,'lon'=4] {'tm'}, dimensions={0} | all-to-all | bytes 4718592 | tf_op jit(solution)/shard_map/all_to_all | solution.py:46
  493.8 59.4 %all_to_all.68 = bf16[16,4,18432]{2,1,0:T(4,128)(2,1)S(1)} all-to-all(bf16[16,4,18432]{2,1,0:T(4,128)(2,1)S(1)} %broadcast_in_dim.28), channel_id=1, replica_groups=mesh['tm'=16,'lat'=4,'lon'=4] {'tm'}, dimensions={0} | all-to-all | bytes 4718592 | tf_op jit(solution)/shard_map/all_to_all | solution.py:13
  558.1 5.7 div.53
  563.8 7.6 %fusion.51 = f32[64,64]{1,0:T(8,128)S(1)} fusion(f32[64,18432]{1,0:T(8,128)} %div.53), kind=kOutput, calls=%fused_computation.80 | convolution fusion | flops 905969664 | bytes 4734976 | tf_op jit(solution)/shard_map/dot_general | solution.py:79
  572.6 5.3 all-to-all-start.11
  577.9 4.3 reshape.106
  586.8 5.8 cholesky.81
  594.0 4.9 custom-call.11
  598.9 7.9 %convolution_convert_fusion = bf16[64,18432]{1,0:T(8,128)(2,1)} fusion(f32[64,18432]{1,0:T(8,128)} %reshape.106, f32[18432]{0:T(1024)S(1)} %fusion.27, f32[1,64,64]{1,2,0:T(8,128)S(1)} %custom-call.11), kind=kOutput, calls=%fused_computation.1 | convolution fusion | flops 909508608 | bytes 7168000 | tf_op jit(solution)/shard_map/triangular_solve/dot.1 | solution.py:82
  (79 shorter events, 71.0 us)
Async XLA Ops:
  0.6 1.7 copy-start
  155.1 1.4 copy-start.2
  174.4 15.5 %all-to-all-start.3 = ((f32[16,1,4096]{2,1,0:T(1,128)}), f32[16,1,4096]{2,1,0:T(1,128)S(1)}, u32[]{:S(2)}, u32[]{:S(2)}) async-start(f32[16,1,4096]{2,1,0:T(1,128)} %reshape.121), calls=%async_computation.3 | async-start | bytes 524288 | tf_op jit(solution)/shard_map/all_to_all | solution.py:13
  355.6 1.4 copy-start.3
  375.0 12.7 %all-to-all-start.7 = ((f32[16,1,4096]{2,1,0:T(1,128)}), f32[16,1,4096]{2,1,0:T(1,128)S(1)}, u32[]{:S(2)}, u32[]{:S(2)}) async-start(f32[16,1,4096]{2,1,0:T(1,128)} %reshape.125), calls=%async_computation.7 | async-start | bytes 524288 | tf_op jit(solution)/shard_map/all_to_all | solution.py:13
  553.2 1.4 copy-start.1
  572.6 12.6 %all-to-all-start.11 = ((f32[16,1,4096]{2,1,0:T(1,128)}), f32[16,1,4096]{2,1,0:T(1,128)S(1)}, u32[]{:S(2)}, u32[]{:S(2)}) async-start(f32[16,1,4096]{2,1,0:T(1,128)} %reshape.129), calls=%async_computation.11 | async-start | bytes 524288 | tf_op jit(solution)/shard_map/all_to_all | solution.py:13
where the time goes:
time: 619 us; the launch traced here: 609 us
  blocking collectives  402 us (65%)
  other arithmetic  63.1 us (10%)
  local copies, waits for them, and re-layouts  59.1 us (10%)
  matrix products  54.8 us (9%)
  starting transfers between devices  18.6 us (3%)
  waiting for transfers between devices  9.13 us (1%)
    all_to_all x6, blocking collectives, sent_to_all(): lax.all_to_all(jnp.broadcast_to(shard[None], (count, *shard.shape)), axis...  210 us
    all_to_all x3, blocking collectives, sum_at_owner(): lax.all_to_all(parts, axis, split_axis=0, concat_axis=0, tiled=True)  192 us
    dot_general x3, matrix products, local(): local_gram = jnp.dot(image, image.T, precision=lax.Precision.HIGHEST)  22.9 us
    another operation x3, matrix products, local(): lax.linalg.triangular_solve(factor, image, left_side=True, lower=True)  21.3 us
    another operation x9, other arithmetic, local(): factor = jnp.linalg.cholesky(gram_sum)  19.6 us
    all_to_all x3, starting transfers between devices, sent_to_all(): lax.all_to_all(jnp.broadcast_to(shard[None], (count, *shard.shape)), axis...  18.6 us
    div x3, local copies, waits for them, and re-layouts, local(): image = summed * weight_row / total_hours  17.2 us
    another operation x6, other arithmetic, local(): lax.linalg.triangular_solve(factor, image, left_side=True, lower=True)  16.6 us
  transfers between devices with their start and end apart: 3, of which 3 were waited for; matrix products, arithmetic and copies ran while one was open for 2% of the time, Pallas kernels for 0%

commit v1 on v0

v1 whole, which is shorter than its diff:
```python
import jax
import jax.numpy as jnp
from jax import lax
from jax.sharding import PartitionSpec as P

ITERS = 3
NLAT = 384
NLON = 768
GRID = ("lat", "lon")
EXACT = lax.Precision.HIGHEST


def exchanged(parts, axes):
    return lax.all_to_all(parts, axes, split_axis=0, concat_axis=0, tiled=True)


def from_all(shard, axes):
    count = lax.axis_size(axes)
    return exchanged(jnp.broadcast_to(shard[None], (count, *shard.shape)), axes)


def row_weight(global_point):
    lat_index = global_point // NLON
    latitude = (-90.0 + 180.0 * (lat_index.astype(jnp.float32) + 0.5) / NLAT) * (jnp.pi / 180.0)
    return jnp.sqrt(jnp.cos(latitude))


def sum_everywhere(values):
    count = lax.axis_size(GRID)
    lines, rank = values.shape
    mine = exchanged(values.reshape(count, lines // count, rank), GRID).sum(axis=0)
    mine = from_all(mine, "tm").sum(axis=0)
    return from_all(mine, GRID).reshape(lines, rank)


def lower_inverse(factor):
    unit = jnp.eye(factor.shape[0], dtype=jnp.float32)
    return lax.linalg.triangular_solve(factor, unit, left_side=True, lower=True)


def local(anomaly, start_basis):
    hour_rows, points = anomaly.shape
    rank = start_basis.shape[0]
    groups = lax.axis_size("tm")
    hours = hour_rows * groups
    part = points // groups
    block_start = (lax.axis_index("lat") * lax.axis_size("lon") + lax.axis_index("lon")) * points
    weight_row = row_weight(block_start + jnp.arange(points, dtype=jnp.int32))
    weight_part = lax.dynamic_slice_in_dim(weight_row, lax.axis_index("tm") * part, part)

    parts = jnp.moveaxis(anomaly.reshape(hour_rows, groups, part), 1, 0)
    fields = exchanged(parts, "tm").reshape(hours, part)

    scaled = (start_basis.astype(jnp.float32) * weight_row).astype(jnp.bfloat16)
    first = lax.dot_general(
        anomaly, scaled, (((1,), (1,)), ((), ())), preferred_element_type=jnp.float32
    )
    first = from_all(first, GRID).sum(axis=0).astype(jnp.bfloat16)
    coeffs = from_all(first, "tm").reshape(hours, rank)

    for iteration in range(ITERS):
        image = lax.dot_general(
            coeffs, fields, (((0,), (0,)), ((), ())), preferred_element_type=jnp.float32
        )
        image = image * weight_part / hours
        gram = jnp.dot(image, image.T, precision=EXACT)
        if iteration == ITERS - 1:
            break
        scaled = (image * weight_part).astype(jnp.bfloat16)
        raw = lax.dot_general(
            fields, scaled, (((1,), (1,)), ((), ())), preferred_element_type=jnp.float32
        )
        total = sum_everywhere(jnp.concatenate([raw, gram], axis=0))
        factor = jnp.linalg.cholesky(total[hours:])
        inverse = lower_inverse(factor)
        coeffs = jnp.dot(total[:hours], inverse.T, precision=EXACT).astype(jnp.bfloat16)

    gathered = lax.all_gather(image.astype(jnp.bfloat16), "tm", axis=0, tiled=False)
    gram = from_all(from_all(gram, GRID).sum(axis=0), "tm").sum(axis=0)
    factor = jnp.linalg.cholesky(gram)
    inverse = lower_inverse(factor)
    whole = jnp.moveaxis(gathered, 0, 1).reshape(rank, points)
    current = jnp.dot(inverse, whole.astype(jnp.float32), precision=EXACT)
    return (current.astype(jnp.bfloat16), jnp.diagonal(factor))


def solution(mesh):
    in_specs = (P("tm", ("lat", "lon")), P(None, ("lat", "lon")))
    out_specs = (P(None, ("lat", "lon")), P())
    return jax.shard_map(local, mesh=mesh, in_specs=in_specs, out_specs=out_specs, check_vma=False)
```

time: 619 us -> 313 us (0.51); the launches traced: 609 us -> 312 us
  blocking collectives: 402 us -> 131 us
  waiting for transfers between devices: 9.13 us -> 83.6 us
  local copies, waits for them, and re-layouts: 59.1 us -> 12 us
  matrix products: 54.8 us -> 13.2 us
  other arithmetic: 63.1 us -> 40.8 us
  between operations: 1.46 us -> 14.5 us
    all_to_all x9 -> x8, blocking collectives: 402 us -> 131 us  [exchanged(): return lax.all_to_all(parts, axes, split_axis=0, concat_axis=0, tiled=True)]
    all_to_all x3, waiting for transfers between devices: 9.13 us -> 75.1 us  [exchanged(): return lax.all_to_all(parts, axes, split_axis=0, concat_axis=0, tiled=True)]
    another operation x3, matrix products: 21.3 us -> 0.74 us  [lower_inverse(): return lax.linalg.triangular_solve(factor, unit, left_side=True, lower=True)]
    dot_general x6 -> x11, matrix products: 29.6 us -> 9.31 us  [the longest x1 3.38 us: local(): current = jnp.dot(inverse, whole.astype(jnp.float32), precision=EXACT)]
    div x3 -> x0, local copies, waits for them, and re-layouts: 17.2 us -> none  [local(): image = summed * weight_row / total_hours]
    convert_element_type x3 -> x1, local copies, waits for them, and re-layouts: 13 us -> 0.09 us  [local(): first = from_all(first, GRID).sum(axis=0).astype(jnp.bfloat16)]
    div x6 -> x3, other arithmetic: 10.5 us -> 0.03 us  [the longest x2 0.02 us: local(): factor = jnp.linalg.cholesky(total[hours:])]
    reshape x3 -> x7, local copies, waits for them, and re-layouts: 12.7 us -> 3.44 us  [the longest x1 1.75 us: local(): parts = jnp.moveaxis(anomaly.reshape(hour_rows, groups, part), 1, 0)]
  transfers between devices with their start and end apart: 3 -> 4, of which waited for: 3 -> 4; matrix products, arithmetic and copies ran while one was open for 2% -> 7% of each run, Pallas kernels for 0% -> 0%
where the time goes in v1:
time: 313 us; the launch traced here: 312 us
  blocking collectives  131 us (42%)
  waiting for transfers between devices  83.6 us (27%)
  other arithmetic  40.8 us (13%)
  starting transfers between devices  17.3 us (6%)
  between operations  14.5 us (5%)
  matrix products  13.2 us (4%)
  local copies, waits for them, and re-layouts  12 us (4%)
    all_to_all x8, blocking collectives, exchanged(): return lax.all_to_all(parts, axes, split_axis=0, concat_axis=0, tiled=True)  131 us
    all_to_all x3, waiting for transfers between devices, exchanged(): return lax.all_to_all(parts, axes, split_axis=0, concat_axis=0, tiled=True)  75.1 us
    all_to_all x3, starting transfers between devices, exchanged(): return lax.all_to_all(parts, axes, split_axis=0, concat_axis=0, tiled=True)  17.3 us
    another operation x6, other arithmetic, lower_inverse(): return lax.linalg.triangular_solve(factor, unit, left_side=True, lower=True)  16.6 us
    another operation x6, other arithmetic, local(): factor = jnp.linalg.cholesky(total[hours:])  13 us
    all_gather x1, waiting for transfers between devices, local(): lax.all_gather(image.astype(jnp.bfloat16), 'tm', axis=0, tiled=False)  8.44 us
    another operation x3, other arithmetic, local(): factor = jnp.linalg.cholesky(gram)  6.52 us
  transfers between devices with their start and end apart: 4, of which 4 were waited for; matrix products, arithmetic and copies ran while one was open for 7% of the time, Pallas kernels for 0%

profile of v1, /device:TPU:1, one launch (start us, length us, event | category | flops | bytes accessed | tf_op | source)
XLA Modules:
  0.0 312.0 jit_solution(12235002605996548691)
XLA Ops:
  7.5 3.2 %fusion.4 = f32[64,64]{0,1:T(8,128)S(1)} fusion(bf16[64,18432]{1,0:T(8,128)(2,1)} %param.5, bf16[64,18432]{1,0:T(8,128)(2,1)} %param.6, f32[18432]{0:T(1024)S(1)} %fusion.21), kind=kOutput, calls=%fused_computation.15 | convolution fusion | flops 154533888 | bytes 4808704 | tf_op jit(solution)/shard_map/dot_general | solution.py:55
  11.1 14.5 %all_to_all.55 = f32[16,1,4096]{2,1,0:T(1,128)S(1)} all-to-all(f32[16,1,4096]{2,1,0:T(1,128)S(1)} %reshape.92), channel_id=1, replica_groups=mesh['tm'=16,'lat'=4,'lon'=4] {'lat','lon'}, dimensions={0} | all-to-all | bytes 524288 | tf_op jit(solution)/shard_map/all_to_all | solution.py:14
  26.2 1.3 reduce.4
  27.9 0.9 reshape.94
  28.8 10.0 %all-to-all-start.1 = ((bf16[16,2,2048]{2,1,0:T(2,128)(2,1)}), bf16[16,2,2048]{2,1,0:T(2,128)(2,1)S(1)}, u32[]{:S(2)}, u32[]{:S(2)}) async-start(bf16[16,2,2048]{2,1,0:T(2,128)(2,1)} %reshape.94), calls=%async_computation.1 | async-start | bytes 262144 | tf_op jit(solution)/shard_map/all_to_all | solution.py:14
  38.8 1.7 copy.45
  40.5 8.6 %all-to-all-done.1 = bf16[16,2,2048]{2,1,0:T(2,128)(2,1)S(1)} async-done(((bf16[16,2,2048]{2,1,0:T(2,128)(2,1)}), bf16[16,2,2048]{2,1,0:T(2,128)(2,1)S(1)}, u32[]{:S(2)}, u32[]{:S(2)}) %all-to-all-start.1) | async-done | bytes 131104 | tf_op jit(solution)/shard_map/all_to_all | solution.py:14
  49.1 3.7 %all-to-all-start.2 = ((bf16[16,64,1152]{2,1,0:T(8,128)(2,1)}), bf16[16,64,1152]{2,1,0:T(8,128)(2,1)S(1)}, u32[]{:S(2)}, u32[]{:S(2)}) async-start(bf16[16,64,1152]{2,1,0:T(8,128)(2,1)} %bitcast.84), calls=%async_computation.2 | async-start | bytes 4718592 | tf_op jit(solution)/shard_map/all_to_all | solution.py:14
  53.2 54.7 %all-to-all-done.2 = bf16[16,64,1152]{2,1,0:T(8,128)(2,1)S(1)} async-done(((bf16[16,64,1152]{2,1,0:T(8,128)(2,1)}), bf16[16,64,1152]{2,1,0:T(8,128)(2,1)S(1)}, u32[]{:S(2)}, u32[]{:S(2)}) %all-to-all-start.2) | async-done | bytes 2359328 | tf_op jit(solution)/shard_map/all_to_all | solution.py:14
  110.4 16.2 %all_to_all.56 = f32[16,68,64]{1,2,0:T(8,128)S(1)} all-to-all(f32[16,68,64]{1,2,0:T(8,128)S(1)} %copy.29), channel_id=1, replica_groups=mesh['tm'=16,'lat'=4,'lon'=4] {'lat','lon'}, dimensions={0} | all-to-all | bytes 557056 | tf_op jit(solution)/shard_map/all_to_all | solution.py:14
  126.7 22.7 %all_to_all.57 = f32[16,68,64]{1,2,0:T(8,128)S(1)} all-to-all(f32[16,68,64]{1,2,0:T(8,128)S(1)} %broadcast_in_dim.21), channel_id=1, replica_groups=mesh['tm'=16,'lat'=4,'lon'=4] {'tm'}, dimensions={0} | all-to-all | bytes 557056 | tf_op jit(solution)/shard_map/all_to_all | solution.py:14
  149.5 15.4 %all_to_all.58 = f32[16,68,64]{1,2,0:T(8,128)S(1)} all-to-all(f32[16,68,64]{1,2,0:T(8,128)S(1)} %broadcast_in_dim.22), channel_id=1, replica_groups=mesh['tm'=16,'lat'=4,'lon'=4] {'lat','lon'}, dimensions={0} | all-to-all | bytes 557056 | tf_op jit(solution)/shard_map/all_to_all | solution.py:14
  165.6 5.8 %cholesky.59 = f32[64,64]{1,0:T(8,128)S(1)} custom-call(f32[64,64]{1,0:T(8,128)S(1)} %fusion.36), custom_call_target="Cholesky" | custom-call | tf_op jit(solution)/shard_map/jit(cholesky)/cholesky | solution.py:74
  172.8 4.9 %custom-call.9 = f32[1,64,64]{1,2,0:T(8,128)S(1)} custom-call(f32[1,64,64]{2,1,0:T(8,128)S(1)} %fusion.29), custom_call_target="InvertDiagBlocksLowerTriangular" | custom-call | tf_op jit(solution)/shard_map/triangular_solve/custom-call.0 | solution.py:38
  180.8 13.5 %all_to_all.59 = f32[16,68,64]{1,2,0:T(8,128)S(1)} all-to-all(f32[16,68,64]{1,2,0:T(8,128)S(1)} %copy.33), channel_id=1, replica_groups=mesh['tm'=16,'lat'=4,'lon'=4] {'lat','lon'}, dimensions={0} | all-to-all | bytes 557056 | tf_op jit(solution)/shard_map/all_to_all | solution.py:14
  194.3 19.7 %all_to_all.60 = f32[16,68,64]{1,2,0:T(8,128)S(1)} all-to-all(f32[16,68,64]{1,2,0:T(8,128)S(1)} %broadcast_in_dim.23), channel_id=1, replica_groups=mesh['tm'=16,'lat'=4,'lon'=4] {'tm'}, dimensions={0} | all-to-all | bytes 557056 | tf_op jit(solution)/shard_map/all_to_all | solution.py:14
  214.1 16.2 %all_to_all.61 = f32[16,68,64]{1,2,0:T(8,128)S(1)} all-to-all(f32[16,68,64]{1,2,0:T(8,128)S(1)} %broadcast_in_dim.24), channel_id=1, replica_groups=mesh['tm'=16,'lat'=4,'lon'=4] {'lat','lon'}, dimensions={0} | all-to-all | bytes 557056 | tf_op jit(solution)/shard_map/all_to_all | solution.py:14
  231.0 5.8 %cholesky.70 = f32[64,64]{1,0:T(8,128)S(1)} custom-call(f32[64,64]{1,0:T(8,128)S(1)} %fusion.34), custom_call_target="Cholesky" | custom-call | tf_op jit(solution)/shard_map/jit(cholesky)/cholesky | solution.py:74
  238.1 4.9 %custom-call.10 = f32[1,64,64]{1,2,0:T(8,128)S(1)} custom-call(f32[1,64,64]{2,1,0:T(8,128)S(1)} %fusion.30), custom_call_target="InvertDiagBlocksLowerTriangular" | custom-call | tf_op jit(solution)/shard_map/triangular_solve/custom-call.0 | solution.py:38
  243.7 1.2 fusion.45
  245.7 12.3 %all_to_all.62 = f32[16,1,4096]{2,1,0:T(1,128)S(1)} all-to-all(f32[16,1,4096]{2,1,0:T(1,128)S(1)} %reshape.96), channel_id=1, replica_groups=mesh['tm'=16,'lat'=4,'lon'=4] {'lat','lon'}, dimensions={0} | all-to-all | bytes 524288 | tf_op jit(solution)/shard_map/all_to_all | solution.py:14
  258.0 1.3 reduce.5
  259.6 1.0 reshape.98
  260.6 3.5 %all-to-all-start.10 = ((f32[16,1,4096]{2,1,0:T(1,128)}), f32[16,1,4096]{2,1,0:T(1,128)S(1)}, u32[]{:S(2)}, u32[]{:S(2)}) async-start(f32[16,1,4096]{2,1,0:T(1,128)} %reshape.98), calls=%async_computation.10 | async-start | bytes 524288 | tf_op jit(solution)/shard_map/all_to_all | solution.py:14
  264.2 11.8 %all-to-all-done.10 = f32[16,1,4096]{2,1,0:T(1,128)S(1)} async-done(((f32[16,1,4096]{2,1,0:T(1,128)}), f32[16,1,4096]{2,1,0:T(1,128)S(1)}, u32[]{:S(2)}, u32[]{:S(2)}) %all-to-all-start.10) | async-done | bytes 262176 | tf_op jit(solution)/shard_map/all_to_all | solution.py:14
  276.0 1.3 reduce.6
  277.7 5.8 %cholesky.81 = f32[64,64]{1,0:T(8,128)S(1)} custom-call(f32[64,64]{1,0:T(8,128)S(1)} %fusion.32), custom_call_target="Cholesky" | custom-call | tf_op jit(solution)/shard_map/jit(cholesky)/cholesky | solution.py:80
  284.9 4.9 %custom-call.11 = f32[1,64,64]{1,2,0:T(8,128)S(1)} custom-call(f32[1,64,64]{2,1,0:T(8,128)S(1)} %get-tuple-element.4), custom_call_target="InvertDiagBlocksLowerTriangular" | custom-call | tf_op jit(solution)/shard_map/triangular_solve/custom-call.0 | solution.py:38
  289.8 1.3 gather_fusion
  291.3 8.4 %all-gather.3.cloned.1.call-done = bf16[1024,1152]{1,0:T(8,128)(2,1)} async-done(((bf16[64,1152]{1,0:T(8,128)(2,1)}), bf16[1024,1152]{1,0:T(8,128)(2,1)}) %all-gather.3.cloned.1.call-update) | async-done | bytes 2359312 | tf_op jit(solution)/shard_map/all_gather | solution.py:78
  299.8 2.0 copy.42
  301.7 3.4 %convolution_convert_fusion = bf16[64,18432]{1,0:T(8,128)(2,1)} fusion(f32[64,64]{1,0:T(8,128)S(1)} %fusion.23, bf16[64,18432]{1,0:T(8,128)(2,1)S(1)} %bitcast.85), kind=kOutput, calls=%fused_computation.1 | convolution fusion | flops 907149312 | bytes 4734976 | tf_op jit(solution)/shard_map/dot_general | solution.py:83
  (70 shorter events, 15.4 us)
Async XLA Ops:
  10.7 28.0 %copy-start = (bf16[64,18432]{1,0:T(8,128)(2,1)S(1)}, bf16[64,18432]{1,0:T(8,128)(2,1)}, u32[]{:S(2)}) copy-start(bf16[64,18432]{1,0:T(8,128)(2,1)} %param.5) | copy-start | bytes 7077892
  28.8 20.4 %all-to-all-start.1 = ((bf16[16,2,2048]{2,1,0:T(2,128)(2,1)}), bf16[16,2,2048]{2,1,0:T(2,128)(2,1)S(1)}, u32[]{:S(2)}, u32[]{:S(2)}) async-start(bf16[16,2,2048]{2,1,0:T(2,128)(2,1)} %reshape.94), calls=%async_computation.1 | async-start | bytes 262144 | tf_op jit(solution)/shard_map/all_to_all | solution.py:14
  49.1 58.8 %all-to-all-start.2 = ((bf16[16,64,1152]{2,1,0:T(8,128)(2,1)}), bf16[16,64,1152]{2,1,0:T(8,128)(2,1)S(1)}, u32[]{:S(2)}, u32[]{:S(2)}) async-start(bf16[16,64,1152]{2,1,0:T(8,128)(2,1)} %bitcast.84), calls=%async_computation.2 | async-start | bytes 4718592 | tf_op jit(solution)/shard_map/all_to_all | solution.py:14
  52.9 246.9 %all-gather.3.cloned.1.call-start = ((), (), s32[]{:S(2)}) async-start(), calls=%async_computation.11 | async-start | bytes 2506752 | tf_op jit(solution)/shard_map/all_gather | solution.py:78
  260.6 15.4 %all-to-all-start.10 = ((f32[16,1,4096]{2,1,0:T(1,128)}), f32[16,1,4096]{2,1,0:T(1,128)S(1)}, u32[]{:S(2)}, u32[]{:S(2)}) async-start(f32[16,1,4096]{2,1,0:T(1,128)} %reshape.98), calls=%async_computation.10 | async-start | bytes 524288 | tf_op jit(solution)/shard_map/all_to_all | solution.py:14
Sparse Core Ops, SparseCore 0:
  245.0 54.6 all-gather.2
